TPU v7x, 32 devices: a whole 2x2x4 slice. The times are simulated.
32 devices in a mesh: rep: 8 (over z, y), shard: 4 (over x, core).
Axes of the slice: x: 2, y: 2, z: 4, core: 2. Of those that a mesh axis runs over, the one named last changes fastest.
Arguments:
- prompt: bfloat16 [8, 1024, 768], P('rep', 'shard'), may hold values from -6 to 6
- conts: bfloat16 [8, 4, 512, 768], P('rep', 'shard'), may hold values from -6 to 6
- prompt_cot: bfloat16 [8, 1024, 768], P('rep', 'shard'), may hold values from -6 to 6
- cont_cot: bfloat16 [8, 4, 512, 768], P('rep', 'shard'), may hold values from -6 to 6
- labels: int32 [8, 4], P('rep', 'shard'), may hold values from 0 to 13
- w_qkv: float32 [768, 2304], P('shard'), may hold values from -0.21875 to 0.21875
- w_out: float32 [768, 768], P('shard'), may hold values from -3.5 to 3.5
- w_in: float32 [768, 3072], P('shard'), may hold values from -0.21875 to 0.21875
- w_ffo: float32 [3072, 768], P('shard'), may hold values from -0.109375 to 0.109375
- layer_biases: float32 [6, 768], replicated, may hold values from -3 to 3
- norm_gains: float32 [2, 768], replicated, may hold values from 0.25 to 1.75
- bias_in: float32 [3072], replicated, may hold values from -3 to 3
- w_student: float32 [768, 128], replicated, may hold values from -0.21875 to 0.21875
- student_vectors: float32 [3, 128], replicated, may hold values from -4 to 4
- w_pool: float32 [128, 128], replicated, may hold values from -0.5 to 0.5
- w_class: float32 [128, 14], replicated, may hold values from -1 to 1
- bias_class: float32 [14], replicated, may hold values from -3 to 3
Outputs:
- prompt_out: bfloat16 [8, 1024, 768], P('rep', 'shard')
- cont_out: bfloat16 [8, 4, 512, 768], P('rep', 'shard')
- logits: float32 [8, 4, 14], P('rep', 'shard')
- prompt_grad: float32 [8, 1024, 768], P('rep', 'shard')
- cont_grad: float32 [8, 4, 512, 768], P('rep', 'shard')
- grad_qkv: float32 [768, 2304], P('shard')
- grad_out: float32 [768, 768], P('shard')
- grad_in: float32 [768, 3072], P('shard')
- grad_ffo: float32 [3072, 768], P('shard')
- grad_biases: float32 [6, 768], replicated
- grad_gains: float32 [2, 768], replicated
- grad_bias_in: float32 [3072], replicated
- grad_student: float32 [768, 128], replicated
- grad_student_vectors: float32 [3, 128], replicated
- grad_pool: float32 [128, 128], replicated
- grad_class: float32 [128, 14], replicated
- grad_bias_class: float32 [14], replicated
All inputs are finite; a program needn't handle non-finite values.
Results may differ from a plain program's by a relative error of at most 0.02.
Values may be sent and summed in bfloat16 or wider, within the bound.
A program may use at most 192 MiB of HBM per device.

v0:
```python
import jax
import jax.numpy as jnp
from jax import lax
from jax.sharding import PartitionSpec as P

D = 768
HEADS = 12
DH = 64
STU = 128
SHEADS = 2
HIGHEST = lax.Precision.HIGHEST
NEG_BIG = -1e30


def dot_plain(left, right):
    return jnp.dot(left, right, preferred_element_type=jnp.float32)


def dot_first(left, right):
    return lax.dot_general(
        left, right, (((0,), (0,)), ((), ())), preferred_element_type=jnp.float32
    )


def dot_second(left, right):
    return lax.dot_general(
        left, right, (((1,), (1,)), ((), ())), preferred_element_type=jnp.float32
    )


def column_slice(matrix, head_index):
    return lax.dynamic_slice_in_dim(matrix, head_index * DH, DH, 1)


def layer_norm(values, gain, shift):
    center = values - jnp.mean(values, -1, keepdims=True)
    spread = jnp.mean(center * center, -1, keepdims=True)
    return center * lax.rsqrt(spread + 1e-05) * gain + shift


def gelu_exact(values):
    return jax.nn.gelu(values, approximate=False)


def attend_forward(queries, keys_all, values_all, allowed):
    scaling = DH ** (-0.5)

    def one_head(head_index):
        scores = jnp.where(
            allowed,
            dot_second(column_slice(queries, head_index), column_slice(keys_all, head_index))
            * scaling,
            NEG_BIG,
        )
        largest = jnp.max(scores, 1, keepdims=True)
        expo = jnp.exp(scores - largest)
        total = jnp.sum(expo, 1, keepdims=True)
        probs = (expo / total).astype(jnp.bfloat16)
        return (
            dot_plain(probs, column_slice(values_all, head_index)),
            (largest + jnp.log(total))[:, 0],
        )

    heads, log_totals = lax.map(one_head, jnp.arange(HEADS))
    return (heads.transpose(1, 0, 2).reshape(queries.shape[0], HEADS * DH), log_totals)


def attend_backward(queries, keys_all, values_all, allowed, grad_att, log_totals):
    scaling = DH ** (-0.5)

    def one_head(item):
        head_index, log_row = item
        query_h = column_slice(queries, head_index)
        key_h = column_slice(keys_all, head_index)
        grad_h = column_slice(grad_att, head_index)
        scores = jnp.where(allowed, dot_second(query_h, key_h) * scaling, NEG_BIG)
        probs = jnp.exp(scores - log_row[:, None])
        grad_probs = dot_second(grad_h, column_slice(values_all, head_index))
        delta = jnp.sum(grad_probs * probs, 1, keepdims=True)
        grad_scores = (probs * (grad_probs - delta)).astype(jnp.bfloat16)
        grad_query = dot_plain(grad_scores, key_h) * scaling
        grad_key = dot_first(grad_scores, query_h) * scaling
        grad_value = dot_first(probs.astype(jnp.bfloat16), grad_h)
        return (grad_query, grad_key, grad_value)

    grad_q, grad_k, grad_v = lax.map(one_head, (jnp.arange(HEADS), log_totals))

    def merge_heads(block):
        return block.transpose(1, 0, 2).reshape(block.shape[1], HEADS * DH)

    return (merge_heads(grad_q), merge_heads(grad_k), merge_heads(grad_v))


def student_loss(stu_rows, pool_query, bias_pool, w_pool, w_class, bias_class, label_value):
    part_w = STU // SHEADS
    parts = stu_rows.reshape(stu_rows.shape[0], SHEADS, part_w)
    queries = pool_query.reshape(SHEADS, part_w)
    scores = jnp.einsum("tha,ha->ht", parts, queries, precision=HIGHEST) * part_w ** (-0.5)
    largest = jnp.max(scores, -1, keepdims=True)
    expo = jnp.exp(scores - largest)
    weights = expo / jnp.sum(expo, -1, keepdims=True)
    pooled = jnp.einsum("ht,tha->ha", weights, parts, precision=HIGHEST).reshape(STU)
    top_layer = jnp.tanh(jnp.dot(pooled, w_pool, precision=HIGHEST) + bias_pool)
    logit_row = jnp.dot(top_layer, w_class, precision=HIGHEST) + bias_class
    top_logit = jnp.max(logit_row)
    log_total = jnp.log(jnp.sum(jnp.exp(logit_row - top_logit))) + top_logit
    picked = jnp.sum(jnp.where(jnp.arange(logit_row.shape[0]) == label_value, logit_row, 0.0))
    return (log_total - picked, logit_row)


def body(
    prompt,
    conts,
    prompt_cot,
    cont_cot,
    labels,
    w_qkv,
    w_out,
    w_in,
    w_ffo,
    layer_biases,
    norm_gains,
    bias_in,
    w_student,
    student_vectors,
    w_pool,
    w_class,
    bias_class,
):
    prompt_rows = prompt.shape[1]
    cont_len = conts.shape[2]
    prompt_len = prompt_rows * lax.axis_size("shard")
    qkv_low = w_qkv.astype(jnp.bfloat16)
    out_low = w_out.astype(jnp.bfloat16)
    in_low = w_in.astype(jnp.bfloat16)
    ffo_low = w_ffo.astype(jnp.bfloat16)
    qkv_full, out_full, in_full, ffo_full = (
        lax.all_gather(qkv_low, "shard", axis=0, tiled=True),
        lax.all_gather(out_low, "shard", axis=0, tiled=True),
        lax.all_gather(in_low, "shard", axis=0, tiled=True),
        lax.all_gather(ffo_low, "shard", axis=0, tiled=True),
    )
    tokens = jnp.concatenate([prompt[0], conts[0, 0]], 0)
    tokens_f = tokens.astype(jnp.float32)
    zero_row = jnp.zeros((D,), jnp.float32)
    bias_three = jnp.concatenate([layer_biases[0], zero_row, layer_biases[1]])
    qkv_b = (dot_plain(tokens, qkv_full) + bias_three).astype(jnp.bfloat16)
    queries = qkv_b[:, :D]
    keys_own = qkv_b[:, D : 2 * D]
    values_own = qkv_b[:, 2 * D :]
    prompt_keys, prompt_values = (
        lax.all_gather(keys_own[:prompt_rows], "shard", axis=0, tiled=True),
        lax.all_gather(values_own[:prompt_rows], "shard", axis=0, tiled=True),
    )
    keys_all = jnp.concatenate([prompt_keys, keys_own[prompt_rows:]], 0)
    values_all = jnp.concatenate([prompt_values, values_own[prompt_rows:]], 0)
    key_pos = jnp.arange(prompt_len + cont_len)
    query_pos = jnp.concatenate(
        [
            lax.axis_index("shard") * prompt_rows + jnp.arange(prompt_rows),
            prompt_len + jnp.arange(cont_len),
        ]
    )
    allowed = key_pos[None, :] <= query_pos[:, None]
    attended, log_totals = attend_forward(queries, keys_all, values_all, allowed)
    att_b = attended.astype(jnp.bfloat16)
    branch = dot_plain(att_b, out_full) + layer_biases[2]
    resid_one = tokens_f + branch
    first = layer_norm(resid_one, norm_gains[0], layer_biases[4])
    first_b = first.astype(jnp.bfloat16)
    hidden = dot_plain(first_b, in_full) + bias_in
    act_b = gelu_exact(hidden).astype(jnp.bfloat16)
    ffn = dot_plain(act_b, ffo_full) + layer_biases[3]
    resid_two = first + ffn
    output = layer_norm(resid_two, norm_gains[1], layer_biases[5])
    output_b = output.astype(jnp.bfloat16)
    cont_b = output_b[prompt_rows:]
    student_low = w_student.astype(jnp.bfloat16)
    stu = dot_plain(cont_b, student_low) + student_vectors[0]

    def loss_closed(stu_rows, pool_query, bias_pool, pool_weight, class_weight, class_bias):
        return student_loss(
            stu_rows, pool_query, bias_pool, pool_weight, class_weight, class_bias, labels[0, 0]
        )

    loss_value, loss_pull, logit_row = jax.vjp(
        loss_closed,
        stu,
        student_vectors[1],
        student_vectors[2],
        w_pool,
        w_class,
        bias_class,
        has_aux=True,
    )
    g_stu, g_query, g_pbias, g_pool, g_class, g_cbias = loss_pull(jnp.ones((), jnp.float32))
    g_stu_b = g_stu.astype(jnp.bfloat16)
    g_sbias = jnp.sum(g_stu_b.astype(jnp.float32), 0)
    g_student = dot_first(cont_b, g_stu_b)
    student_back = dot_second(g_stu_b, student_low)
    g_output = jnp.concatenate([prompt_cot[0], cont_cot[0, 0]], 0).astype(jnp.float32)
    g_output = g_output + jnp.concatenate(
        [jnp.zeros((prompt_rows, D), jnp.float32), student_back], 0
    )
    qkv_back, out_back, in_back, ffo_back = (
        lax.all_gather(qkv_low, "shard", axis=0, tiled=True),
        lax.all_gather(out_low, "shard", axis=0, tiled=True),
        lax.all_gather(in_low, "shard", axis=0, tiled=True),
        lax.all_gather(ffo_low, "shard", axis=0, tiled=True),
    )
    norm_two, norm_two_pull = jax.vjp(layer_norm, resid_two, norm_gains[1], layer_biases[5])
    g_resid_two, g_gain_two, g_shift_two = norm_two_pull(g_output)
    g_ffn_b = g_resid_two.astype(jnp.bfloat16)
    g_ffo = dot_first(act_b, g_ffn_b)
    g_ffo_bias = jnp.sum(g_ffn_b.astype(jnp.float32), 0)
    g_act = dot_second(g_ffn_b, ffo_back)
    gelu_value, gelu_pull = jax.vjp(gelu_exact, hidden)
    g_hidden_b = gelu_pull(g_act)[0].astype(jnp.bfloat16)
    g_in = dot_first(first_b, g_hidden_b)
    g_in_bias = jnp.sum(g_hidden_b.astype(jnp.float32), 0)
    g_first = g_resid_two + dot_second(g_hidden_b, in_back)
    norm_one, norm_one_pull = jax.vjp(layer_norm, resid_one, norm_gains[0], layer_biases[4])
    g_resid_one, g_gain_one, g_shift_one = norm_one_pull(g_first)
    g_branch_b = g_resid_one.astype(jnp.bfloat16)
    g_outw = dot_first(att_b, g_branch_b)
    g_out_bias = jnp.sum(g_branch_b.astype(jnp.float32), 0)
    g_att_b = dot_second(g_branch_b, out_back).astype(jnp.bfloat16)
    g_query_rows, g_keys_all, g_values_all = attend_backward(
        queries, keys_all, values_all, allowed, g_att_b, log_totals
    )
    query_grad_b = g_query_rows.astype(jnp.bfloat16)
    cont_kv_b = jnp.concatenate([g_keys_all[prompt_len:], g_values_all[prompt_len:]], 1).astype(
        jnp.bfloat16
    )
    block_kv_b = jnp.concatenate([g_keys_all[:prompt_len], g_values_all[:prompt_len]], 1).astype(
        jnp.bfloat16
    )
    kv_weights = qkv_back[:, D:]
    g_query_w = dot_first(tokens, query_grad_b)
    g_kv_w = dot_first(tokens[prompt_rows:], cont_kv_b)
    g_tokens = g_resid_one + dot_second(query_grad_b, qkv_back[:, :D])
    cont_through = dot_second(cont_kv_b, kv_weights)
    kv_summed = lax.psum_scatter(
        block_kv_b.astype(jnp.float32).astype(jnp.bfloat16),
        "shard",
        scatter_dimension=0,
        tiled=True,
    ).astype(jnp.float32)
    g_kv_w = g_kv_w + lax.dot_general(
        tokens_f[:prompt_rows],
        kv_summed,
        (((0,), (0,)), ((), ())),
        precision=HIGHEST,
        preferred_element_type=jnp.float32,
    )
    prompt_through = jnp.dot(
        kv_summed,
        kv_weights.astype(jnp.float32).T,
        precision=HIGHEST,
        preferred_element_type=jnp.float32,
    )
    value_cols = jnp.sum(kv_summed[:, D:], 0)
    g_tokens = g_tokens + jnp.concatenate([prompt_through, cont_through], 0)
    g_qkvw = jnp.concatenate([g_query_w, g_kv_w], 1)
    g_query_bias = jnp.sum(query_grad_b.astype(jnp.float32), 0)
    g_value_bias = jnp.sum(cont_kv_b[:, D:].astype(jnp.float32), 0) + value_cols
    owned = (
        lax.psum_scatter(
            g_qkvw.astype(jnp.bfloat16), "shard", scatter_dimension=0, tiled=True
        ).astype(jnp.float32),
        lax.psum_scatter(
            g_outw.astype(jnp.bfloat16), "shard", scatter_dimension=0, tiled=True
        ).astype(jnp.float32),
        lax.psum_scatter(
            g_in.astype(jnp.bfloat16), "shard", scatter_dimension=0, tiled=True
        ).astype(jnp.float32),
        lax.psum_scatter(
            g_ffo.astype(jnp.bfloat16), "shard", scatter_dimension=0, tiled=True
        ).astype(jnp.float32),
    )
    owned_qkv, owned_out, owned_in, owned_ffo = (
        lax.psum(owned[0].astype(jnp.bfloat16), "rep").astype(jnp.float32),
        lax.psum(owned[1].astype(jnp.bfloat16), "rep").astype(jnp.float32),
        lax.psum(owned[2].astype(jnp.bfloat16), "rep").astype(jnp.float32),
        lax.psum(owned[3].astype(jnp.bfloat16), "rep").astype(jnp.float32),
    )
    g_biases = jnp.stack(
        [g_query_bias, g_value_bias, g_out_bias, g_ffo_bias, g_shift_one, g_shift_two]
    )
    g_gains = jnp.stack([g_gain_one, g_gain_two])
    g_vectors = jnp.stack([g_sbias, g_query, g_pbias])
    summed = lax.psum(
        (g_biases, g_gains, g_in_bias, g_student, g_vectors, g_pool, g_class, g_cbias),
        ("rep", "shard"),
    )
    return (
        output_b[:prompt_rows][None],
        output_b[prompt_rows:][None, None],
        logit_row[None, None],
        g_tokens[:prompt_rows][None],
        g_tokens[prompt_rows:][None, None],
        owned_qkv,
        owned_out,
        owned_in,
        owned_ffo,
        summed[0],
        summed[1],
        summed[2],
        summed[3],
        summed[4],
        summed[5],
        summed[6],
        summed[7],
    )


def solution(mesh):
    return jax.shard_map(
        body,
        mesh=mesh,
        in_specs=(
            P("rep", "shard", None),
            P("rep", "shard", None, None),
            P("rep", "shard", None),
            P("rep", "shard", None, None),
            P("rep", "shard"),
            P("shard", None),
            P("shard", None),
            P("shard", None),
            P("shard", None),
            P(),
            P(),
            P(),
            P(),
            P(),
            P(),
            P(),
            P(),
        ),
        out_specs=(
            P("rep", "shard", None),
            P("rep", "shard", None, None),
            P("rep", "shard", None),
            P("rep", "shard", None),
            P("rep", "shard", None, None),
            P("shard", None),
            P("shard", None),
            P("shard", None),
            P("shard", None),
            P(),
            P(),
            P(),
            P(),
            P(),
            P(),
            P(),
            P(),
        ),
        check_vma=False,
    )
```

profile of v0, /device:TPU:1, one launch (start us, length us, event | category | flops | bytes accessed | tf_op | source)
XLA Modules:
  0.0 1008.6 jit_solution(7969806802003201834)
XLA Ops:
  10.5 33.0 %all-gather.7.cloned.1.call-done = bf16[768,2304]{1,0:T(8,128)(2,1)} async-done(((bf16[192,2304]{1,0:T(8,128)(2,1)}), bf16[768,2304]{1,0:T(8,128)(2,1)}) %all-gather.7.cloned.1.call-update) | async-done | bytes 3538960 | tf_op jit(solution)/shard_map/all_gather | solution.py:138
  43.5 5.3 add_convert_fusion.1
  65.2 6.2 all-gather.11.cloned.1.call-done
  73.2 20.0 %all-gather.9.cloned.1.call-done = bf16[1024,768]{1,0:T(8,128)(2,1)} async-done(((bf16[256,768]{1,0:T(8,128)(2,1)}), bf16[1024,768]{1,0:T(8,128)(2,1)}) %all-gather.9.cloned.1.call-update) | async-done | bytes 1572880 | tf_op jit(solution)/shard_map/all_gather | solution.py:152
  97.5 133.8 %while.28 = (s32[]{:T(128)}, bf16[12,768,64]{1,2,0:T(8,128)(2,1)}, f32[12,768]{1,0:T(8,128)}, s32[12]{0:T(128)S(1)}, bf16[768,768]{1,0:T(8,128)(2,1)}, /*index=5...) while((s32[]{:T(128)}, bf16[12,768,64]{1,2,0:T(8,128)(2,1)}, ...), condition=%wide.region_3.4_spmd.clone, body=%wide.region_0.3_spmd.clone.sunk | while | flops 312605952 | bytes 34253524 | solution.py:64
  104.5 4.1 fusion.160
  115.6 4.1 fusion.160
  137.9 4.1 fusion.160
  149.0 4.1 fusion.160
  160.1 4.6 fusion.160
  171.7 4.1 fusion.160
  182.8 4.2 fusion.160
  193.9 4.1 fusion.160
  205.0 4.1 fusion.160
  216.1 4.1 fusion.160
  227.2 4.1 fusion.160
  236.7 29.4 %multiply_convert_fusion.1 = (bf16[768,3072]{1,0:T(8,128)(2,1)}, f32[768,3072]{1,0:T(8,128)}, f32[768,3072]{1,0:T(8,128)}) fusion(f32[3072]{0:T(1024)S(1)} %copy-done.42, bf16[768,3072]{1,0:T(8,128)(2,1)} %all-gather.15.cloned.1.call-done, f32[768,768]{0,1:T(8,128)S(1)} %get-tuple-element.319, f32[768]{0:T(1024)S(1)} %get-tuple-element.226, ...), kind=kOutput, calls=%fused_computation.48 | convolution fusion | flops 3782541312 | bytes 30695424 | tf_op jit(solution)/shard_map/dot_general | solution.py:16
  266.1 8.7 fusion.101
  294.3 13.0 %convert_reduce_fusion = (f32[3072]{0:T(1024)S(1)}, bf16[768,3072]{1,0:T(8,128)(2,1)S(1)}) fusion(f32[768,3072]{1,0:T(8,128)} %get-tuple-element.302, f32[768,3072]{1,0:T(8,128)} %get-tuple-element.320, f32[3072]{0:T(1024)S(1)} %copy-done.43, bf16[768,768]{0,1:T(8,128)(2,1)S(1)} %get-tuple-element.288, bf16[3072,768]{1,0:T(8,128)(2,1)} %all-gather.17.cloned.1.call-done), kind=kOutput, calls=%fused_computation.46 | convolution fusion | flops 3663983616 | bytes 29515776 | tf_op jit(solution)/shard_map/dot_general | solution.py:26
  307.3 4.5 multiply_reduce_fusion.2
  317.2 168.6 %while.29 = (s32[]{:T(128)}, bf16[12,768,64]{1,2,0:T(8,128)(2,1)}, bf16[12,1536,64]{1,2,0:T(8,128)(2,1)}, bf16[12,1536,64]{1,2,0:T(8,128)(2,1)}, s32[12]{0:T(128...) while((s32[]{:T(128)}, bf16[12,768,64]{1,2,0:T(8,128)(2,1)}, ...), condition=%wide.region_23.24_spmd.clone, body=%wide.region_21.23_spmd.clone.sunk | while | flops 766917888 | bytes 38360792 | solution.py:86
  496.9 32.2 %reduce-scatter.8.cloned.1.call-done = bf16[256,1536]{0,1:T(8,128)(2,1)} async-done(((bf16[1024,1536]{0,1:T(8,128)(2,1)}), bf16[256,1536]{0,1:T(8,128)(2,1)}) %reduce-scatter.8.cloned.1.call-update) | async-done | bytes 786448 | tf_op jit(solution)/shard_map/reduce_scatter | solution.py:243
  534.6 5.8 copy.89
  544.3 9.7 convolution_convert_fusion.1
  554.1 8.7 convolution_convert_fusion
  562.9 18.1 %reduce-scatter.16.cloned.1.call-done = bf16[192,2304]{1,0:T(8,128)(2,1)} async-done(((bf16[768,2304]{1,0:T(8,128)(2,1)}), bf16[192,2304]{1,0:T(8,128)(2,1)}) %reduce-scatter.16.cloned.1.call-update) | async-done | bytes 884752
  583.3 26.6 %reduce-scatter.10.cloned.1.call-done = bf16[192,768]{1,0:T(8,128)(2,1)} async-done(((bf16[768,768]{1,0:T(8,128)(2,1)}), bf16[192,768]{1,0:T(8,128)(2,1)}) %reduce-scatter.10.cloned.1.call-update) | async-done | bytes 294928 | tf_op jit(solution)/shard_map/reduce_scatter | solution.py:271
  609.9 50.4 %reduce-scatter.12.cloned.1.call-done = bf16[192,3072]{1,0:T(8,128)(2,1)} async-done(((bf16[768,3072]{1,0:T(8,128)(2,1)}), bf16[192,3072]{1,0:T(8,128)(2,1)}) %reduce-scatter.12.cloned.1.call-update) | async-done | bytes 1179664 | tf_op jit(solution)/shard_map/reduce_scatter | solution.py:274
  660.3 50.4 %reduce-scatter.14.cloned.1.call-done = bf16[768,768]{1,0:T(8,128)(2,1)} async-done(((bf16[3072,768]{1,0:T(8,128)(2,1)}), bf16[768,768]{1,0:T(8,128)(2,1)}) %reduce-scatter.14.cloned.1.call-update) | async-done | bytes 1179664 | tf_op jit(solution)/shard_map/reduce_scatter | solution.py:277
  736.4 43.8 %all-reduce.1 = (f32[6,768]{1,0:T(8,128)}, f32[2,768]{1,0:T(2,128)}, f32[3072]{0:T(1024)}, f32[3,128]{1,0:T(4,128)}, f32[128,14]{0,1:T(8,128)}, /*index=5*/f32[14]{0:T(128)}) all-reduce(f32[6,768]{1,0:T(8,128)S(1)} %stack.32, f32[2,768]{1,0:T(2,128)S(1)} %pad_maximum_fusion.11, ...), channel_id=1, replica_groups=mesh['rep'=8,'shard'=4] {'rep','shard'}, use_global_device_ids=true, to_apply=%region_40.41 | all-reduce | flops 11406 | bytes 91248 | tf_op jit(solution)/shard_map/psum | solution.py:292
  780.2 85.0 %all-reduce.9.cloned.1.call-done = (bf16[192,2304]{0,1:T(8,128)(2,1)}, bf16[192,768]{1,0:T(8,128)(2,1)}, bf16[192,3072]{1,0:T(8,128)(2,1)}, bf16[768,768]{1,0:T(8,128)(2,1)}) async-done(((bf16[192,2304]{0,1:T(8,128)(2,1)}, bf16[192,768]{1,0:T(8,128)(2,1)}, bf16[192,3072]{1,0:T(8,128)(2,1)}, bf16[768,768]{1,0:T(8,128)(2,1)}), (bf16[192,2304]{0,1:T(8,128)(2,1)}, bf16[192,768]{1,0:T(8,128)(2,1)}, ...) | async-done | bytes 3538960 | tf_op jit(solution)/shard_map/psum | solution.py:282
  872.3 126.1 %all-reduce.7.cloned.1.call-done = (f32[768,128]{1,0:T(8,128)}, f32[128,128]{1,0:T(8,128)}) async-done(((f32[768,128]{1,0:T(8,128)}, f32[128,128]{1,0:T(8,128)}), (f32[768,128]{1,0:T(8,128)}, f32[128,128]{1,0:T(8,128)})) %all-reduce.7.cloned.1.call-update) | async-done | bytes 458768 | tf_op jit(solution)/shard_map/psum | solution.py:292
  (439 shorter events, 351.7 us)
Async XLA Ops:
  7.2 271.8 %copy-start = (f32[128,128]{1,0:T(8,128)S(1)}, f32[128,128]{1,0:T(8,128)}, u32[]{:S(2)}) copy-start(f32[128,128]{1,0:T(8,128)} %param.35) | copy-start | bytes 196612
  7.2 36.3 %all-gather.7.cloned.1.call-start = ((), (), s32[]{:S(2)}) async-start(), calls=%async_computation.5 | async-start | bytes 4423680 | tf_op jit(solution)/shard_map/all_gather | solution.py:138
  9.9 61.5 %all-gather.11.cloned.1.call-start = ((), (), s32[]{:S(2)}) async-start(), calls=%async_computation.7 | async-start | bytes 1966080 | tf_op jit(solution)/shard_map/all_gather | solution.py:153
  10.2 33.3 %copy-start.27 = (bf16[1,1,512,768]{2,3,1,0:T(8,128)(2,1)}, bf16[1,1,512,768]{2,3,1,0:T(8,128)(2,1)S(1)}, u32[]{:S(2)}) copy-start(bf16[1,1,512,768]{2,3,1,0:T(8,128)(2,1)S(1)} %copy.63) | copy-start | bytes 2359300
  10.4 33.1 %copy-start.31 = (bf16[1,256,768]{1,2,0:T(8,128)(2,1)}, bf16[1,256,768]{1,2,0:T(8,128)(2,1)S(1)}, u32[]{:S(2)}) copy-start(bf16[1,256,768]{1,2,0:T(8,128)(2,1)S(1)} %copy.62) | copy-start | bytes 1179652
  43.5 8.8 copy-start.29
  51.6 41.6 %all-gather.9.cloned.1.call-start = ((), (), s32[]{:S(2)}) async-start(), calls=%async_computation.6 | async-start | bytes 1966080 | tf_op jit(solution)/shard_map/all_gather | solution.py:152
  52.3 179.1 %all-gather.13.cloned.1.call-start = ((), (), s32[]{:S(2)}) async-start(), calls=%async_computation.8 | async-start | bytes 1474560 | tf_op jit(solution)/shard_map/all_gather | solution.py:139
  53.1 183.2 %all-gather.15.cloned.1.call-start = ((), (), s32[]{:S(2)}) async-start(), calls=%async_computation.9 | async-start | bytes 5898240 | tf_op jit(solution)/shard_map/all_gather | solution.py:140
  54.4 4.5 copy-start.26
  54.4 4.8 copy-start.30
  54.4 211.7 %all-gather.17.cloned.1.call-start = ((), (), s32[]{:S(2)}) async-start(), calls=%async_computation.10 | async-start | bytes 5898240 | tf_op jit(solution)/shard_map/all_gather | solution.py:141
  57.4 471.7 %reduce-scatter.8.cloned.1.call-start = ((), (), s32[]{:S(2)}) async-start(), calls=%async_computation.11 | async-start | bytes 3932160 | tf_op jit(solution)/shard_map/reduce_scatter | solution.py:243
  235.9 30.1 %copy-start.6 = (f32[768,768]{0,1:T(8,128)}, f32[768,768]{0,1:T(8,128)S(1)}, u32[]{:S(2)}) copy-start(f32[768,768]{0,1:T(8,128)S(1)} %get-tuple-element.319) | copy-start | bytes 7077892
  275.1 4.0 copy-start.35
  280.6 4.5 copy-start.39
  287.5 4.3 copy-start.11
  293.6 13.7 %slice-start = ((s8[4718592]{0:T(1024)(128)(4,1)}), s8[4194304]{0:T(1024)(128)(4,1)S(1)}, s32[]{:S(2)}) async-start(s8[4718592]{0:T(1024)(128)(4,1)} %bitcast.224), calls=%async_computation.18 | async-start | bytes 8388608
  293.9 13.4 %copy-start.19 = (bf16[768,768]{0,1:T(8,128)(2,1)}, bf16[768,768]{0,1:T(8,128)(2,1)S(1)}, u32[]{:S(2)}) copy-start(bf16[768,768]{0,1:T(8,128)(2,1)S(1)} %get-tuple-element.288) | copy-start | bytes 3538948
  294.3 13.0 %copy-start.7 = (f32[768,768]{0,1:T(8,128)S(1)}, f32[768,768]{0,1:T(8,128)}, u32[]{:S(2)}) copy-start(f32[768,768]{0,1:T(8,128)} %copy-done.6) | copy-start | bytes 7077892
  294.3 13.1 %slice-start.1 = ((s8[4718592]{0:T(1024)(128)(4,1)}), s8[524288]{0:T(1024)(128)(4,1)S(1)}, s32[]{:S(2)}) async-start(s8[4718592]{0:T(1024)(128)(4,1)} %bitcast.224), calls=%async_computation.19 | async-start | bytes 1048576
  307.3 4.6 copy-start.44
  491.0 90.0 %reduce-scatter.16.cloned.1.call-start = ((), (), s32[]{:S(2)}) async-start(), calls=%async_computation.15 | async-start | bytes 4423680
  491.3 3.5 copy-start.4
  540.4 69.5 %reduce-scatter.10.cloned.1.call-start = ((), (), s32[]{:S(2)}) async-start(), calls=%async_computation.12 | async-start | bytes 1474560 | tf_op jit(solution)/shard_map/reduce_scatter | solution.py:271
  544.2 116.1 %reduce-scatter.12.cloned.1.call-start = ((), (), s32[]{:S(2)}) async-start(), calls=%async_computation.13 | async-start | bytes 5898240 | tf_op jit(solution)/shard_map/reduce_scatter | solution.py:274
  554.1 156.7 %reduce-scatter.14.cloned.1.call-start = ((), (), s32[]{:S(2)}) async-start(), calls=%async_computation.14 | async-start | bytes 5898240 | tf_op jit(solution)/shard_map/reduce_scatter | solution.py:277
  562.9 302.3 %all-reduce.9.cloned.1.call-start = ((), (), s32[]{:S(2)}) async-start(), calls=%async_computation.17 | async-start | bytes 7667712 | tf_op jit(solution)/shard_map/psum | solution.py:282
  710.8 287.6 %all-reduce.7.cloned.1.call-start = ((), (), s32[]{:S(2)}) async-start(), calls=%async_computation.16 | async-start | bytes 917504 | tf_op jit(solution)/shard_map/psum | solution.py:292
  715.4 7.0 copy-start.24
  724.7 3.6 copy-start.33
  869.8 131.9 %copy-start.1 = (f32[128,128]{1,0:T(8,128)S(1)}, f32[128,128]{1,0:T(8,128)}, u32[]{:S(2)}) copy-start(f32[128,128]{1,0:T(8,128)} %param.35) | copy-start | bytes 196612
  (39 other events, 83.1 us)
Sparse Core Ops, SparseCore 0:
  10.2 33.2 all-gather.6
  51.7 19.6 all-gather.10
  73.5 19.6 all-gather.8
  95.2 17.4 all-gather.12
  114.7 37.4 all-gather.14
  153.6 37.4 all-gather.16
  491.1 37.8 reduce-scatter.7
  540.5 40.4 reduce-scatter.15
  584.1 25.7 reduce-scatter.9
  612.5 47.8 reduce-scatter.11
  662.9 47.8 reduce-scatter.13
  715.7 149.3 all-reduce.8
  872.0 126.3 all-reduce.6
where the time goes:
time: 1020 us; the launch traced here: 1010 us
  waiting for transfers between devices  449 us (44%)
  matrix products  322 us (32%)
  local copies, waits for them, and re-layouts  108 us (11%)
  other arithmetic  50.7 us (5%)
  blocking collectives  43.8 us (4%)
  between operations  17.9 us (2%)
  loops' own time  16.2 us (2%)
    dot_general x29, matrix products, dot_plain(): return jnp.dot(left, right, preferred_element_type=jnp.float32)  127 us
    psum x1, waiting for transfers between devices, body(): lax.psum((g_biases, g_gains, g_in_bias, g_student, g_vectors, g_pool, g_c...  126 us
    dot_general x42, matrix products, dot_second(): lax.dot_general(left, right, (((1,), (1,)), ((), ())), preferred_element_...  107 us
    psum x1, waiting for transfers between devices, body(): lax.psum(owned[0].astype(jnp.bfloat16), 'rep').astype(jnp.float32)  85 us
    dot_general x30, matrix products, dot_first(): lax.dot_general(left, right, (((0,), (0,)), ((), ())), preferred_element_...  82.1 us
    reduce_scatter x1, waiting for transfers between devices, body(): lax.psum_scatter(g_ffo.astype(jnp.bfloat16), 'shard', scatter_dimension=0...  50.4 us
    reduce_scatter x1, waiting for transfers between devices, body(): lax.psum_scatter(g_in.astype(jnp.bfloat16), 'shard', scatter_dimension=0,...  50.4 us
    psum x1, blocking collectives, body(): lax.psum((g_biases, g_gains, g_in_bias, g_student, g_vectors, g_pool, g_c...  43.8 us
  transfers between devices with their start and end apart: 13, of which 10 were waited for; matrix products, arithmetic and copies ran while one was open for 22% of the time, Pallas kernels for 0%

commit v1 on v0

--- a/solution.py
+++ b/solution.py
@@ -134,8 +134,33 @@
     out_low = w_out.astype(jnp.bfloat16)
     in_low = w_in.astype(jnp.bfloat16)
     ffo_low = w_ffo.astype(jnp.bfloat16)
+
+    def set_space(field):
+        p_next = jax.lax.axis_size("shard")
+        carry_in, arr_now, z2 = (p_next, jax.lax.axis_index("shard"), field.shape[0])
+        w_next = tuple(
+            (src_i * carry_in if h == 0 else src_i for h, src_i in enumerate(field.shape))
+        )
+        u1 = jnp.zeros(w_next, field.dtype)
+        next_value = lax.dynamic_update_slice_in_dim(u1, field, arr_now * z2, axis=0)
+        y_new = local_next = field
+        for dev_j in range(1, carry_in // 2 + 1):
+            w1 = tuple(((h, (h + 1) % carry_in) for h in range(carry_in)))
+            y_new = jax.lax.ppermute(y_new, "shard", w1)
+            next_value = lax.dynamic_update_slice_in_dim(
+                next_value, y_new, (arr_now - dev_j) % carry_in * z2, axis=0
+            )
+            if 2 * dev_j < carry_in:
+                local_next = jax.lax.ppermute(
+                    local_next, "shard", tuple(((h, (h - 1) % carry_in) for h in range(carry_in)))
+                )
+                next_value = lax.dynamic_update_slice_in_dim(
+                    next_value, local_next, (arr_now + dev_j) % carry_in * z2, axis=0
+                )
+        return next_value
+
     qkv_full, out_full, in_full, ffo_full = (
-        lax.all_gather(qkv_low, "shard", axis=0, tiled=True),
+        set_space(qkv_low),
         lax.all_gather(out_low, "shard", axis=0, tiled=True),
         lax.all_gather(in_low, "shard", axis=0, tiled=True),
         lax.all_gather(ffo_low, "shard", axis=0, tiled=True),

time: 1020 us -> 1060 us (1.039)
  waiting for transfers between devices: 449 us -> 470 us
    ppermute x0 -> x3, waiting for transfers between devices: none -> 22.5 us  [the longest x2 22.5 us: set_space(): y_new = jax.lax.ppermute(y_new, 'shard', w1)]
    all_gather x1, waiting for transfers between devices: 33 us -> 18.9 us  [body(): lax.all_gather(qkv_low, 'shard', axis=0, tiled=True)]
    psum x1, waiting for transfers between devices: 85 us -> 96.4 us  [body(): lax.psum(owned[0].astype(jnp.bfloat16), 'rep').astype(jnp.float32)]
    unnamed x105 -> x109, local copies, waits for them, and re-layouts: 30.3 us -> 33 us
  transfers between devices with their start and end apart: 13 -> 16, of which waited for: 10 -> 12; matrix products, arithmetic and copies ran while one was open for 22% -> 22% of each run, Pallas kernels for 0% -> 0%
where the time goes in v1:
time: 1060 us; the launch traced here: 1040 us
  waiting for transfers between devices  470 us (44%)
  matrix products  322 us (30%)
  local copies, waits for them, and re-layouts  118 us (11%)
  other arithmetic  49.2 us (5%)
  blocking collectives  45.4 us (4%)
  between operations  17.8 us (2%)
  loops' own time  16.2 us (2%)
    dot_general x29, matrix products, dot_plain(): return jnp.dot(left, right, preferred_element_type=jnp.float32)  127 us
    psum x1, waiting for transfers between devices, body(): lax.psum((g_biases, g_gains, g_in_bias, g_student, g_vectors, g_pool, g_c...  126 us
    dot_general x42, matrix products, dot_second(): lax.dot_general(left, right, (((1,), (1,)), ((), ())), preferred_element_...  107 us
    psum x1, waiting for transfers between devices, body(): lax.psum(owned[0].astype(jnp.bfloat16), 'rep').astype(jnp.float32)  96.4 us
    dot_general x30, matrix products, dot_first(): lax.dot_general(left, right, (((0,), (0,)), ((), ())), preferred_element_...  82.2 us
    reduce_scatter x1, waiting for transfers between devices, body(): lax.psum_scatter(g_ffo.astype(jnp.bfloat16), 'shard', scatter_dimension=0...  50.6 us
    reduce_scatter x1, waiting for transfers between devices, body(): lax.psum_scatter(g_in.astype(jnp.bfloat16), 'shard', scatter_dimension=0,...  50.3 us
    psum x1, blocking collectives, body(): lax.psum((g_biases, g_gains, g_in_bias, g_student, g_vectors, g_pool, g_c...  45.4 us
  transfers between devices with their start and end apart: 16, of which 12 were waited for; matrix products, arithmetic and copies ran while one was open for 22% of the time, Pallas kernels for 0%

profile of v1, /device:TPU:1, one launch (start us, length us, event | category | flops | bytes accessed | tf_op | source)
XLA Modules:
  0.0 1044.4 jit_solution(5081713423551176880)
XLA Ops:
  13.0 19.4 %collective-permute-done = bf16[192,2304]{1,0:T(8,128)(2,1)S(1)} collective-permute-done((bf16[192,2304]{1,0:T(8,128)(2,1)S(1)}, bf16[192,2304]{1,0:T(8,128)(2,1)S(1)}, u32[]{:S(2)}, u32[]{:S(2)}) %collective-permute-start) | collective-permute-done | bytes 884768 | tf_op jit(solution)/shard_map/ppermute | solution.py:149
  45.9 5.3 add_convert_fusion.1
  67.9 7.5 all-gather.9.cloned.1.call-done
  77.2 20.0 %all-gather.7.cloned.1.call-done = bf16[1024,768]{1,0:T(8,128)(2,1)} async-done(((bf16[256,768]{1,0:T(8,128)(2,1)}), bf16[1024,768]{1,0:T(8,128)(2,1)}) %all-gather.7.cloned.1.call-update) | async-done | bytes 1572880 | tf_op jit(solution)/shard_map/all_gather | solution.py:177
  101.5 133.9 %while.28 = (s32[]{:T(128)}, bf16[12,768,64]{1,2,0:T(8,128)(2,1)}, f32[12,768]{1,0:T(8,128)}, s32[12]{0:T(128)S(1)}, bf16[768,768]{1,0:T(8,128)(2,1)}, /*index=5...) while((s32[]{:T(128)}, bf16[12,768,64]{1,2,0:T(8,128)(2,1)}, ...), condition=%wide.region_3.4_spmd.clone, body=%wide.region_0.3_spmd.clone.sunk | while | flops 312605952 | bytes 34253524 | solution.py:64
  108.5 4.1 fusion.160
  142.0 4.2 fusion.160
  153.1 4.1 fusion.160
  164.2 4.6 fusion.160
  175.8 4.1 fusion.160
  186.9 4.2 fusion.160
  198.0 4.1 fusion.160
  209.1 4.1 fusion.160
  220.2 4.1 fusion.160
  231.3 4.1 fusion.160
  240.7 29.4 %multiply_convert_fusion.1 = (bf16[768,3072]{1,0:T(8,128)(2,1)}, f32[768,3072]{1,0:T(8,128)}, f32[768,3072]{1,0:T(8,128)}) fusion(f32[3072]{0:T(1024)S(1)} %copy-done.44, bf16[768,3072]{1,0:T(8,128)(2,1)} %all-gather.13.cloned.1.call-done, f32[768,768]{0,1:T(8,128)S(1)} %get-tuple-element.321, f32[768]{0:T(1024)S(1)} %get-tuple-element.226, ...), kind=kOutput, calls=%fused_computation.48 | convolution fusion | flops 3782541312 | bytes 30695424 | tf_op jit(solution)/shard_map/dot_general | solution.py:16
  270.1 8.7 fusion.101
  298.3 13.0 %convert_reduce_fusion = (f32[3072]{0:T(1024)S(1)}, bf16[768,3072]{1,0:T(8,128)(2,1)S(1)}) fusion(f32[768,3072]{1,0:T(8,128)} %get-tuple-element.302, f32[768,3072]{1,0:T(8,128)} %get-tuple-element.322, f32[3072]{0:T(1024)S(1)} %copy-done.45, bf16[768,768]{0,1:T(8,128)(2,1)S(1)} %get-tuple-element.288, bf16[3072,768]{1,0:T(8,128)(2,1)} %all-gather.15.cloned.1.call-done), kind=kOutput, calls=%fused_computation.46 | convolution fusion | flops 3663983616 | bytes 29515776 | tf_op jit(solution)/shard_map/dot_general | solution.py:26
  311.4 4.5 multiply_reduce_fusion.2
  321.3 168.7 %while.29 = (s32[]{:T(128)}, bf16[12,768,64]{1,2,0:T(8,128)(2,1)}, bf16[12,1536,64]{1,2,0:T(8,128)(2,1)}, bf16[12,1536,64]{1,2,0:T(8,128)(2,1)}, s32[12]{0:T(128...) while((s32[]{:T(128)}, bf16[12,768,64]{1,2,0:T(8,128)(2,1)}, ...), condition=%wide.region_23.24_spmd.clone, body=%wide.region_21.23_spmd.clone.sunk | while | flops 766917888 | bytes 38360792 | solution.py:86
  501.0 32.0 %reduce-scatter.8.cloned.1.call-done = bf16[256,1536]{0,1:T(8,128)(2,1)} async-done(((bf16[1024,1536]{0,1:T(8,128)(2,1)}), bf16[256,1536]{0,1:T(8,128)(2,1)}) %reduce-scatter.8.cloned.1.call-update) | async-done | bytes 786448 | tf_op jit(solution)/shard_map/reduce_scatter | solution.py:268
  538.5 5.8 copy.89
  548.2 9.4 convolution_convert_fusion
  557.6 9.2 convolution_convert_fusion.1
  567.7 17.2 %reduce-scatter.16.cloned.1.call-done = bf16[192,2304]{1,0:T(8,128)(2,1)} async-done(((bf16[768,2304]{1,0:T(8,128)(2,1)}), bf16[192,2304]{1,0:T(8,128)(2,1)}) %reduce-scatter.16.cloned.1.call-update) | async-done | bytes 884752
  587.2 26.5 %reduce-scatter.10.cloned.1.call-done = bf16[192,768]{1,0:T(8,128)(2,1)} async-done(((bf16[768,768]{1,0:T(8,128)(2,1)}), bf16[192,768]{1,0:T(8,128)(2,1)}) %reduce-scatter.10.cloned.1.call-update) | async-done | bytes 294928 | tf_op jit(solution)/shard_map/reduce_scatter | solution.py:296
  613.8 50.6 %reduce-scatter.14.cloned.1.call-done = bf16[768,768]{1,0:T(8,128)(2,1)} async-done(((bf16[3072,768]{1,0:T(8,128)(2,1)}), bf16[768,768]{1,0:T(8,128)(2,1)}) %reduce-scatter.14.cloned.1.call-update) | async-done | bytes 1179664 | tf_op jit(solution)/shard_map/reduce_scatter | solution.py:302
  664.4 50.3 %reduce-scatter.12.cloned.1.call-done = bf16[192,3072]{1,0:T(8,128)(2,1)} async-done(((bf16[768,3072]{1,0:T(8,128)(2,1)}), bf16[192,3072]{1,0:T(8,128)(2,1)}) %reduce-scatter.12.cloned.1.call-update) | async-done | bytes 1179664 | tf_op jit(solution)/shard_map/reduce_scatter | solution.py:299
  728.6 18.9 %all-gather.17.cloned.1.call-done = bf16[768,2304]{1,0:T(8,128)(2,1)} async-done(((bf16[192,2304]{1,0:T(8,128)(2,1)}), bf16[768,2304]{1,0:T(8,128)(2,1)}) %all-gather.17.cloned.1.call-update) | async-done | bytes 3538960 | tf_op jit(solution)/shard_map/all_gather | solution.py:231
  759.2 45.4 %all-reduce.1 = (f32[6,768]{1,0:T(8,128)}, f32[2,768]{1,0:T(2,128)}, f32[3072]{0:T(1024)}, f32[3,128]{1,0:T(4,128)}, f32[128,14]{0,1:T(8,128)}, /*index=5*/f32[14]{0:T(128)}) all-reduce(f32[6,768]{1,0:T(8,128)S(1)} %stack.32, f32[2,768]{1,0:T(2,128)S(1)} %pad_maximum_fusion.11, ...), channel_id=1, replica_groups=mesh['rep'=8,'shard'=4] {'rep','shard'}, use_global_device_ids=true, to_apply=%region_40.41 | all-reduce | flops 11406 | bytes 91248 | tf_op jit(solution)/shard_map/psum | solution.py:317
  804.6 96.4 %all-reduce.9.cloned.1.call-done = (bf16[192,2304]{0,1:T(8,128)(2,1)}, bf16[192,768]{1,0:T(8,128)(2,1)}, bf16[192,3072]{1,0:T(8,128)(2,1)}, bf16[768,768]{1,0:T(8,128)(2,1)}) async-done(((bf16[192,2304]{0,1:T(8,128)(2,1)}, bf16[192,768]{1,0:T(8,128)(2,1)}, bf16[192,3072]{1,0:T(8,128)(2,1)}, bf16[768,768]{1,0:T(8,128)(2,1)}), (bf16[192,2304]{0,1:T(8,128)(2,1)}, bf16[192,768]{1,0:T(8,128)(2,1)}, ...) | async-done | bytes 3538960 | tf_op jit(solution)/shard_map/psum | solution.py:307
  908.1 126.1 %all-reduce.7.cloned.1.call-done = (f32[768,128]{1,0:T(8,128)}, f32[128,128]{1,0:T(8,128)}) async-done(((f32[768,128]{1,0:T(8,128)}, f32[128,128]{1,0:T(8,128)}), (f32[768,128]{1,0:T(8,128)}, f32[128,128]{1,0:T(8,128)})) %all-reduce.7.cloned.1.call-update) | async-done | bytes 458768 | tf_op jit(solution)/shard_map/psum | solution.py:317
  (453 shorter events, 373.0 us)
Async XLA Ops:
  7.2 275.8 %copy-start = (f32[128,128]{1,0:T(8,128)S(1)}, f32[128,128]{1,0:T(8,128)}, u32[]{:S(2)}) copy-start(f32[128,128]{1,0:T(8,128)} %param.35) | copy-start | bytes 196612
  7.2 68.1 %all-gather.9.cloned.1.call-start = ((), (), s32[]{:S(2)}) async-start(), calls=%async_computation.6 | async-start | bytes 1966080 | tf_op jit(solution)/shard_map/all_gather | solution.py:178
  9.4 25.6 %copy-start.37 = (f32[6,768]{1,0:T(8,128)S(1)}, f32[6,768]{1,0:T(8,128)}, u32[]{:S(2)}) copy-start(f32[6,768]{1,0:T(8,128)} %param.30) | copy-start | bytes 55300
  9.4 26.2 %copy-start.14 = (bf16[1,1,512,768]{3,2,1,0:T(8,128)(2,1)S(1)}, bf16[1,1,512,768]{3,2,1,0:T(8,128)(2,1)}, u32[]{:S(2)}) copy-start(bf16[1,1,512,768]{3,2,1,0:T(8,128)(2,1)} %param.22) | copy-start | bytes 2359300
  10.4 31.4 %copy-start.13 = (bf16[192,2304]{1,0:T(8,128)(2,1)}, bf16[192,2304]{1,0:T(8,128)(2,1)S(1)}, u32[]{:S(2)}) copy-start(bf16[192,2304]{1,0:T(8,128)(2,1)S(1)} %get-tuple-element.304) | copy-start | bytes 2654212
  10.4 22.0 %collective-permute-start = (bf16[192,2304]{1,0:T(8,128)(2,1)S(1)}, bf16[192,2304]{1,0:T(8,128)(2,1)S(1)}, u32[]{:S(2)}, u32[]{:S(2)}) collective-permute-start(bf16[192,2304]{1,0:T(8,128)(2,1)S(1)} %get-tuple-element.304), channel_id=1, source_target_pairs={{0,1},{1,2},{2,3},{3,0},{4,5},{5,6},{6,7},{7,4},{8,9},{9,10},{10,1... | collective-permute-start | bytes 2654216 | tf_op jit(solution)/shard_map/ppermute | solution.py:149
  13.0 26.7 %collective-permute-start.1 = (bf16[192,2304]{1,0:T(8,128)(2,1)S(1)}, bf16[192,2304]{1,0:T(8,128)(2,1)}, u32[]{:S(2)}, u32[]{:S(2)}) collective-permute-start(bf16[192,2304]{1,0:T(8,128)(2,1)S(1)} %get-tuple-element.304), channel_id=1, source_target_pairs={{0,3},{1,0},{2,1},{3,2},{4,7},{5,4},{6,5},{7,6},{8,11},{9,8},{10,9... | collective-permute-start | bytes 2654216 | tf_op jit(solution)/shard_map/ppermute | solution.py:154
  32.4 12.5 %collective-permute-start.2 = (bf16[192,2304]{1,0:T(8,128)(2,1)S(1)}, bf16[192,2304]{1,0:T(8,128)(2,1)S(1)}, u32[]{:S(2)}, u32[]{:S(2)}) collective-permute-start(bf16[192,2304]{1,0:T(8,128)(2,1)S(1)} %collective-permute-done), channel_id=1, source_target_pairs={{0,1},{1,2},{2,3},{3,0},{4,5},{5,6},{6,7},{7,4},{8,9},{9,10},{10,1... | collective-permute-start | bytes 2654216 | tf_op jit(solution)/shard_map/ppermute | solution.py:149
  38.6 7.3 copy-start.28
  38.7 7.2 copy-start.32
  45.9 8.9 copy-start.30
  54.0 43.2 %all-gather.7.cloned.1.call-start = ((), (), s32[]{:S(2)}) async-start(), calls=%async_computation.5 | async-start | bytes 1966080 | tf_op jit(solution)/shard_map/all_gather | solution.py:177
  54.7 180.7 %all-gather.11.cloned.1.call-start = ((), (), s32[]{:S(2)}) async-start(), calls=%async_computation.7 | async-start | bytes 1474560 | tf_op jit(solution)/shard_map/all_gather | solution.py:164
  55.5 184.8 %all-gather.13.cloned.1.call-start = ((), (), s32[]{:S(2)}) async-start(), calls=%async_computation.8 | async-start | bytes 5898240 | tf_op jit(solution)/shard_map/all_gather | solution.py:165
  56.8 4.8 copy-start.31
  56.8 213.3 %all-gather.15.cloned.1.call-start = ((), (), s32[]{:S(2)}) async-start(), calls=%async_computation.9 | async-start | bytes 5898240 | tf_op jit(solution)/shard_map/all_gather | solution.py:166
  59.8 473.1 %reduce-scatter.8.cloned.1.call-start = ((), (), s32[]{:S(2)}) async-start(), calls=%async_computation.11 | async-start | bytes 3932160 | tf_op jit(solution)/shard_map/reduce_scatter | solution.py:268
  101.5 135.3 %copy-start.41 = (f32[768]{0:T(1024)S(1)}, f32[768]{0:T(1024)}, u32[]{:S(2)}) copy-start(f32[768]{0:T(1024)} %get-tuple-element.227) | copy-start | bytes 9220
  240.0 30.1 %copy-start.6 = (f32[768,768]{0,1:T(8,128)}, f32[768,768]{0,1:T(8,128)S(1)}, u32[]{:S(2)}) copy-start(f32[768,768]{0,1:T(8,128)S(1)} %get-tuple-element.321) | copy-start | bytes 7077892
  297.6 13.7 %slice-start = ((s8[4718592]{0:T(1024)(128)(4,1)}), s8[4194304]{0:T(1024)(128)(4,1)S(1)}, s32[]{:S(2)}) async-start(s8[4718592]{0:T(1024)(128)(4,1)} %bitcast.224), calls=%async_computation.18 | async-start | bytes 8388608
  297.9 13.4 %copy-start.20 = (bf16[768,768]{0,1:T(8,128)(2,1)}, bf16[768,768]{0,1:T(8,128)(2,1)S(1)}, u32[]{:S(2)}) copy-start(bf16[768,768]{0,1:T(8,128)(2,1)S(1)} %get-tuple-element.288) | copy-start | bytes 3538948
  298.3 13.1 %copy-start.7 = (f32[768,768]{0,1:T(8,128)S(1)}, f32[768,768]{0,1:T(8,128)}, u32[]{:S(2)}) copy-start(f32[768,768]{0,1:T(8,128)} %copy-done.6) | copy-start | bytes 7077892
  298.3 13.1 %slice-start.1 = ((s8[4718592]{0:T(1024)(128)(4,1)}), s8[524288]{0:T(1024)(128)(4,1)S(1)}, s32[]{:S(2)}) async-start(s8[4718592]{0:T(1024)(128)(4,1)} %bitcast.224), calls=%async_computation.19 | async-start | bytes 1048576
  495.1 89.8 %reduce-scatter.16.cloned.1.call-start = ((), (), s32[]{:S(2)}) async-start(), calls=%async_computation.15 | async-start | bytes 4423680
  544.3 69.4 %reduce-scatter.10.cloned.1.call-start = ((), (), s32[]{:S(2)}) async-start(), calls=%async_computation.12 | async-start | bytes 1474560 | tf_op jit(solution)/shard_map/reduce_scatter | solution.py:296
  548.2 116.2 %reduce-scatter.14.cloned.1.call-start = ((), (), s32[]{:S(2)}) async-start(), calls=%async_computation.14 | async-start | bytes 5898240 | tf_op jit(solution)/shard_map/reduce_scatter | solution.py:302
  557.6 157.1 %reduce-scatter.12.cloned.1.call-start = ((), (), s32[]{:S(2)}) async-start(), calls=%async_computation.13 | async-start | bytes 5898240 | tf_op jit(solution)/shard_map/reduce_scatter | solution.py:299
  566.9 180.6 %all-gather.17.cloned.1.call-start = ((), (), s32[]{:S(2)}) async-start(), calls=%async_computation.10 | async-start | bytes 4423680 | tf_op jit(solution)/shard_map/all_gather | solution.py:231
  567.6 333.4 %all-reduce.9.cloned.1.call-start = ((), (), s32[]{:S(2)}) async-start(), calls=%async_computation.17 | async-start | bytes 7667712 | tf_op jit(solution)/shard_map/psum | solution.py:307
  714.7 319.6 %all-reduce.7.cloned.1.call-start = ((), (), s32[]{:S(2)}) async-start(), calls=%async_computation.16 | async-start | bytes 917504 | tf_op jit(solution)/shard_map/psum | solution.py:317
  719.2 7.1 copy-start.25
  905.7 131.8 %copy-start.1 = (f32[128,128]{1,0:T(8,128)S(1)}, f32[128,128]{1,0:T(8,128)}, u32[]{:S(2)}) copy-start(f32[128,128]{1,0:T(8,128)} %param.35) | copy-start | bytes 196612
  (44 other events, 105.4 us)
Sparse Core Ops, SparseCore 0:
  54.1 21.2 all-gather.8
  77.5 19.6 all-gather.6
  99.3 17.4 all-gather.10
  118.8 37.4 all-gather.12
  157.7 37.4 all-gather.14
  495.2 37.6 reduce-scatter.7
  544.5 40.4 reduce-scatter.15
  588.1 25.6 reduce-scatter.9
  616.5 47.8 reduce-scatter.13
  666.7 47.8 reduce-scatter.11
  716.3 31.1 all-gather.16
  752.5 148.4 all-reduce.8
  907.8 126.3 all-reduce.6
